TPU v7x, 32 devices: a whole 2x2x4 slice. The times are simulated.
32 devices in a mesh: seq: 16 (over z, x, core), head: 2 (over y).
Axes of the slice: x: 2, y: 2, z: 4, core: 2. Of those that a mesh axis runs over, the one named last changes fastest.
Arguments:
- query: bfloat16 [8192, 1024], P('seq', 'head'), may hold values from -6 to 6
- key_rows: bfloat16 [8192, 128], P('seq'), may hold values from -6 to 6
- value_rows: bfloat16 [8192, 128], P('seq'), may hold values from -6 to 6
- output: bfloat16 [8192, 1024], P('seq', 'head'), may hold values from -1.5 to 1.5
- grad_output: bfloat16 [8192, 1024], P('seq', 'head'), may hold values from -144 to 144
- log_norm: float32 [8, 8192], P('head', 'seq'), may hold values from 0.5 to 12
- stripe: int32 [16], replicated, may hold values from 0 to 15, each once
Outputs:
- grad_query: bfloat16 [8192, 1024], P('seq', 'head')
- grad_key: bfloat16 [8192, 128], P(('seq', 'head'))
- grad_value: bfloat16 [8192, 128], P(('seq', 'head'))
Inputs may be any that keep to these rules, and one draw needn't show every extreme that they name: stripe is a permutation of 0 to 15.
All inputs are finite; a program needn't handle non-finite values.
Results may differ from a plain program's by a relative error of at most 0.0051.
Values may be sent and summed in bfloat16 or wider, within the bound.
No kernel may reach another device: no remote copies, remote signals or barrier semaphores. Data moves between devices by JAX's collectives and lax.ppermute only.
A program may use at most 192 MiB of HBM per device.

v0:
```python
import functools

import jax
import jax.numpy as jnp
from jax import lax
from jax.experimental import pallas as pl
from jax.experimental.pallas import tpu as pltpu
from jax.sharding import PartitionSpec as P


LOG2E = 1.4426950408889634
VMEM_LIMIT = 24 << 20
SMEM = pl.BlockSpec(memory_space=pltpu.SMEM)
BACKS = ((0, 0), (2, 2), (4, 4), (6, 6), (0, 8))
NT = (((1,), (1,)), ((), ()))
NN = (((1,), (0,)), ((), ()))


def dot(a, b, dims):
    return lax.dot_general(a, b, dims, preferred_element_type=jnp.float32)


def terms_kernel(plan, place, heads, starts_dq, *refs):
    blocks, groups = plan
    refs = iter(refs)
    opens = next(refs)
    side = lax.axis_index("head")
    odd = lax.rem(lax.axis_index("seq"), 2)
    kv_refs = [next(refs) for _ in range(blocks)]
    query_grad, level = ({g: next(refs) for g in groups} for _ in range(2))
    dq_in = {g: next(refs) for g in groups if not starts_dq[g]}
    dq = {g: next(refs) for g in groups}
    send, keep = next(refs), next(refs)
    keys, values, keys_t, dk, dv = refs
    rows, d = keys.shape
    half = rows // 2
    mine = pl.multiple_of(side * half, half)
    theirs = pl.multiple_of((1 - side) * half, half)

    def take(ref):
        keys[...] = ref[0]
        values[...] = ref[1]

    if len(kv_refs) == 1:
        take(kv_refs[0])
    else:
        for parity, ref in enumerate(kv_refs):
            pl.when(odd == parity)(functools.partial(take, ref))
    keys_t[...] = keys[...].T
    factor = d**-0.5
    dk[...] = jnp.zeros_like(dk)
    dv[...] = jnp.zeros_like(dv)
    ahead = lax.broadcasted_iota(jnp.int32, (half, half), 0) - lax.broadcasted_iota(
        jnp.int32, (half, half), 1
    )

    opened = {g: opens[2 * place + g : 2 * place + g + 1, :] for g in groups}
    written = set()

    def query(h, g, s):
        return query_grad[g][s : s + half, h * d : h * d + d]

    def grad(h, g, s):
        return query_grad[g][s : s + half, (heads + h) * d : (heads + h) * d + d]

    def scores_of(h, g, a, s):
        scores = dot(keys[a : a + half, :], query(h, g, s), NT)
        grad_probs = dot(values[a : a + half, :], grad(h, g, s), NT)
        return scores, grad_probs

    def gradients_of(h, g, a, s, scores, grad_probs):
        cols = slice(h * d, h * d + d)
        spot = slice(s, s + half)
        probs = jnp.exp2(scores * (factor * LOG2E) - level[g][0, h : h + 1, spot] * LOG2E)
        if s == a:
            probs = jnp.where(ahead < opened[g], probs, 0.0)
        grad_scores = (probs * factor) * (grad_probs - level[g][1, h : h + 1, spot])
        grad_scores = grad_scores.astype(jnp.bfloat16)
        dv[a : a + half, :] += dot(probs.astype(jnp.bfloat16), grad(h, g, s), NN)
        dk[a : a + half, :] += dot(grad_scores, query(h, g, s), NN)
        part = dot(keys_t[:, a : a + half], grad_scores, NN)
        before = dq[g] if (h, g, s) in written else dq_in.get(g)
        dq[g][cols, spot] = part if before is None else before[cols, spot] + part
        written.add((h, g, s))

    tiles = [
        (h, g, a, s)
        for h in range(heads)
        for g in groups
        for a in (0, half)
        for s in range(a, rows, half)
    ]
    last = None
    for tile in tiles:
        ready = scores_of(*tile)
        if last is not None:
            gradients_of(*last)
        last = (*tile, *ready)
    gradients_of(*last)
    keep[0] = dk[pl.ds(mine, half), :]
    keep[1] = dv[pl.ds(mine, half), :]
    send[0] = dk[pl.ds(theirs, half), :].astype(jnp.bfloat16)
    send[1] = dv[pl.ds(theirs, half), :].astype(jnp.bfloat16)


def call(kernel, out_shape, operands, specs=None, **options):
    vmem = pl.BlockSpec(memory_space=pltpu.VMEM)
    return pl.pallas_call(
        kernel,
        out_shape=out_shape,
        in_specs=[SMEM if s else vmem for s in specs or [""] * len(operands)],
        out_specs=[vmem] * len(out_shape),
        compiler_params=pltpu.CompilerParams(vmem_limit_bytes=VMEM_LIMIT),
        **options,
    )(*operands)


def delta_kernel(d, stripe, query_grad, output, norm, rows_out, opens):
    rows_out[0] = norm[...]
    heads = norm.shape[0]
    ones = jnp.ones((8, d), jnp.bfloat16)
    for h in range(heads):
        cols = slice(h * d, h * d + d)
        grad = query_grad[:, (heads + h) * d : (heads + h) * d + d].astype(jnp.float32)
        product = grad * output[:, cols].astype(jnp.float32)
        high = product.astype(jnp.bfloat16)
        low = (product - high.astype(jnp.float32)).astype(jnp.bfloat16)
        rows_out[1, h : h + 1, :] = (dot(ones, high, NT) + dot(ones, low, NT))[:1]
    me = lax.axis_index("seq")
    odd = lax.rem(me, 2)
    n = stripe.shape[0]
    for place, (even_back, odd_back) in enumerate(BACKS):
        source = stripe[lax.rem(me - (1 - odd) * even_back - odd * odd_back + n, n)]
        for g, reader in enumerate((me, me + 1 - 2 * odd)):
            is_open = (source <= stripe[reader]).astype(jnp.int32)
            opens[2 * place + g : 2 * place + g + 1, :] = jnp.full((1, opens.shape[1]), is_open)


def query_kernel(heads, mine_ref, theirs_ref, out_ref):
    d = out_ref.shape[1] // heads
    for h in range(heads):
        cols = slice(h * d, h * d + d)
        out_ref[:, cols] = (mine_ref[cols, :] + theirs_ref[cols, :]).T.astype(out_ref.dtype)


def final_kernel(keep_ref, flip_ref, keep8_ref, flip8_ref, *refs):
    *backs, key_ref, value_ref = refs
    twice = (lax.rem(lax.axis_index("seq"), 2) == 0).astype(jnp.float32)
    for i, out in enumerate((key_ref, value_ref)):
        total = keep_ref[i] + flip_ref[i].astype(jnp.float32)
        total += twice * (keep8_ref[i] + flip8_ref[i].astype(jnp.float32))
        for back in backs:
            total += back[i].astype(jnp.float32)
        out[...] = total.astype(out.dtype)


def terms(plan, backs, kvs, opens, query_grad, level, dq_in):
    _, groups = plan
    rows = query_grad[0].shape[0]
    d = kvs[0].shape[-1]
    width = query_grad[0].shape[1] // 2
    heads = width // d
    starts_dq = [x is None for x in dq_in]
    operands = [opens, *kvs]
    for per_group in (query_grad, level):
        operands += [per_group[g] for g in groups]
    aliases = {}
    for place, g in enumerate(groups):
        if dq_in[g] is not None:
            aliases[len(operands)] = place
            operands.append(dq_in[g])
    halves = (2, rows // 2, d)
    out_shape = [jax.ShapeDtypeStruct((width, rows), jnp.float32) for _ in groups]
    out_shape += [jax.ShapeDtypeStruct(halves, jnp.bfloat16), jax.ShapeDtypeStruct(halves, jnp.float32)]
    out = call(
        functools.partial(terms_kernel, plan, BACKS.index(backs), heads, starts_dq),
        out_shape,
        operands,
        input_output_aliases=aliases,
        scratch_shapes=[
            pltpu.VMEM((rows, d), jnp.bfloat16),
            pltpu.VMEM((rows, d), jnp.bfloat16),
            pltpu.VMEM((d, rows), jnp.bfloat16),
            pltpu.VMEM((rows, d), jnp.float32),
            pltpu.VMEM((rows, d), jnp.float32),
        ],
        cost_estimate=pl.CostEstimate(
            flops=len(groups) * heads * rows * rows * d * 8,
            bytes_accessed=4 * rows * width * 2,
            transcendentals=len(groups) * heads * rows * rows,
        ),
    )
    dq = list(dq_in)
    for place, g in enumerate(groups):
        dq[g] = out[place]
    return dq, *out[len(groups) :]


def shards(query, key_rows, value_rows, output, grad_output, log_norm, stripe):
    rows, width = query.shape
    d = key_rows.shape[1]
    heads = width // d
    half = rows // 2
    n = lax.axis_size("seq")

    def shift(x, by, only_odd=False):
        route = [(i, (i + by) % n) for i in range(n) if i % 2 or not only_odd]
        return lax.ppermute(x, "seq", route)

    def flip_core(x):
        return lax.ppermute(x, "seq", [(i, i ^ 1) for i in range(n)])

    def flip_head(x):
        return lax.ppermute(x, "head", [(0, 1), (1, 0)])

    bf16 = functools.partial(jax.ShapeDtypeStruct, dtype=jnp.bfloat16)
    kv = jnp.stack([key_rows, value_rows])
    kv2 = shift(kv, 2)
    kv4 = shift(kv, 4)
    kv6 = shift(kv2, 4)
    kv8 = shift(kv4, 4, only_odd=True)
    query_grad = jnp.concatenate([query, grad_output], axis=1)
    their_query_grad = flip_core(query_grad)
    my_level, opens = call(
        functools.partial(delta_kernel, d),
        [
            jax.ShapeDtypeStruct((2, heads, rows), jnp.float32),
            jax.ShapeDtypeStruct((2 * len(BACKS), half), jnp.int32),
        ],
        [stripe, query_grad, output, log_norm],
        ["smem", "", "", ""],
    )
    args = (
        opens,
        (query_grad, their_query_grad),
        (my_level, flip_core(my_level)),
    )

    def low_sum(keep, flip):
        return (keep + flip.astype(jnp.float32)).astype(jnp.bfloat16)

    both = (0, 1)
    dq = [None, None]
    dq, send0, keep0 = terms((1, (0,)), (0, 0), [kv], *args, dq)
    dq, send2, keep2 = terms((1, both), (2, 2), [kv2], *args, dq)
    flip0, flip2 = flip_head(jnp.stack([send0, send2]))
    dq, send4, keep4 = terms((1, both), (4, 4), [kv4], *args, dq)
    flip4 = flip_head(send4)
    back2 = shift(low_sum(keep2, flip2), -2)
    dq, send6, keep6 = terms((1, both), (6, 6), [kv6], *args, dq)
    flip6 = flip_head(send6)
    back4 = shift(low_sum(keep4, flip4), -4)
    back6 = shift(low_sum(keep6, flip6), -6)
    dq, send8, keep8 = terms((2, (1,)), (0, 8), [kv, kv8], *args, dq)
    flip8 = flip_head(send8)
    their_dq = flip_core(dq[1])
    back8 = shift(low_sum(keep8, flip8), -8, only_odd=True)
    (grad_query,) = call(
        functools.partial(query_kernel, heads), [bf16((rows, width))], [dq[0], their_dq]
    )
    grad_key, grad_value = call(
        final_kernel,
        [bf16((half, d))] * 2,
        [keep0, flip0, keep8, flip8, back2, back4, back6, back8],
    )
    return grad_query, grad_key, grad_value


def solution(mesh):
    placed = (
        P("seq", "head"),
        P("seq", None),
        P("seq", None),
        P("seq", "head"),
        P("seq", "head"),
        P("head", "seq"),
        P(),
    )

    return jax.shard_map(
        shards,
        mesh=mesh,
        in_specs=placed,
        out_specs=(P("seq", "head"), P(("seq", "head"), None), P(("seq", "head"), None)),
        check_vma=False,
    )
```

profile of v0, /device:TPU:31, one launch (start us, length us, event | category | flops | bytes accessed | tf_op | source)
XLA Modules:
  0.0 61.3 jit_solution(2865859594068964274)
XLA Ops:
  0.6 0.0 copy-start.3
  0.6 1.2 %constant_dynamic-update-slice_fusion.1 = bf16[512,1024]{1,0:T(8,128)(2,1)S(1)} fusion(bf16[512,512]{1,0:T(8,128)(2,1)} %param.7), kind=kLoop, calls=%fused_computation.10 | loop fusion | bytes 1048576
  1.8 0.0 copy-done.3
  1.8 0.0 copy-start.4
  1.8 0.0 copy-start.5
  1.8 0.0 copy-start.1
  1.9 0.1 constant_dynamic-update-slice_fusion.query_grad.refs_2_
  1.9 0.0 copy-start
  1.9 0.7 %collective-permute-start.2 = (bf16[512,1024]{1,0:T(8,128)(2,1)S(1)}, bf16[512,1024]{1,0:T(8,128)(2,1)S(1)}, u32[]{:S(2)}, u32[]{:S(2)}) collective-permute-start(bf16[512,1024]{1,0:T(8,128)(2,1)S(1)} %constant_dynamic-update-slice_fusion.query_grad.refs_2_), channel_id=1, source_target_pairs={{0,2},{2,0},{4,6},{6,4},{8,10},{10,8},{12,14},{14,12},{16,18},{18,... | collective-permute-start | bytes 3145736 | tf_op jit(solution)/shard_map/ppermute | solution.py:211
  2.7 0.1 copy-done.4
  2.7 0.1 copy-done.5
  2.8 0.0 copy-start.2
  2.8 0.1 collective-permute-start.4
  2.9 1.2 %collective-permute-start = (bf16[2,512,128]{2,1,0:T(8,128)(2,1)S(1)}, bf16[2,512,128]{2,1,0:T(8,128)(2,1)S(1)}, u32[]{:S(2)}, u32[]{:S(2)}) collective-permute-start(bf16[2,512,128]{2,1,0:T(8,128)(2,1)S(1)} %pad_maximum_fusion.refs_1_), channel_id=1, source_target_pairs={{0,4},{2,6},{4,8},{6,10},{8,12},{10,14},{12,16},{14,18},{16,20},{1... | collective-permute-start | bytes 786440 | tf_op jit(solution)/shard_map/ppermute | solution.py:208
  4.1 0.0 copy-done.1
  4.1 0.0 copy-done
  4.1 0.0 copy-done.2
  4.1 0.9 %shard_map.94 = (f32[2,4,512]{2,1,0:T(4,128)S(1)}, s32[10,256]{1,0:T(8,128)S(1)}) custom-call(s32[16]{0:T(128)S(1)} %copy-done.2, bf16[512,1024]{1,0:T(8,128)(2,1)S(1)} %constant_dynamic-update-slice_fusion.query_grad.refs_2_, bf16[512,512]{1,0:T(8,128)(2,1)S(1)} %copy-done, f32[4,512]{1,0:T(4,128)S(1)} %copy-done.1), custom_call_target="tpu_custom_call" | custom-call | tf_op jit(solution)/shard_map/pallas_call | solution.py:108
  5.0 1.3 %collective-permute-start.3 = (f32[2,4,512]{2,1,0:T(4,128)S(1)}, f32[2,4,512]{2,1,0:T(4,128)S(1)}, u32[]{:S(2)}, u32[]{:S(2)}) collective-permute-start(f32[2,4,512]{2,1,0:T(4,128)S(1)} %get-tuple-element.26.refs_3_.refs_4_), channel_id=1, source_target_pairs={{0,2},{2,0},{4,6},{6,4},{8,10},{10,8},{12,14},{14,12},{16,18},{18,... | collective-permute-start | bytes 49160 | tf_op jit(solution)/shard_map/ppermute | solution.py:211
  6.3 2.2 %shard_map.95 = (f32[512,512]{1,0:T(8,128)S(1)}, bf16[2,256,128]{2,1,0:T(8,128)(2,1)S(1)}, f32[2,256,128]{2,1,0:T(8,128)S(1)}) custom-call(s32[10,256]{1,0:T(8,128)S(1)} %get-tuple-element.25.refs_0_, bf16[2,512,128]{2,1,0:T(8,128)(2,1)S(1)} %pad_maximum_fusion.refs_1_, bf16[512,1024]{1,0:T(8,128)(2,1)S(1)} %constant_dynamic-update-slice_fusion.query_grad.refs_2_, ...), custom_call_target="tpu_custom_call" | custom-call | flops 1073741824 | bytes 2097152 | tf_op jit(solution)/shard_map/pallas_call | solution.py:108
  8.5 1.5 %collective-permute-done.4.refs_1_ = bf16[2,512,128]{2,1,0:T(8,128)(2,1)S(1)} collective-permute-done((bf16[2,512,128]{2,1,0:T(8,128)(2,1)S(1)}, bf16[2,512,128]{2,1,0:T(8,128)(2,1)S(1)}, u32[]{:S(2)}, u32[]{:S(2)}) %collective-permute-start.4) | collective-permute-done | bytes 262176 | tf_op jit(solution)/shard_map/ppermute | solution.py:208
  10.1 3.8 %collective-permute-start.5 = (bf16[2,512,128]{2,1,0:T(8,128)(2,1)S(1)}, bf16[2,512,128]{2,1,0:T(8,128)(2,1)S(1)}, u32[]{:S(2)}, u32[]{:S(2)}) collective-permute-start(bf16[2,512,128]{2,1,0:T(8,128)(2,1)S(1)} %collective-permute-done.4.refs_1_), channel_id=1, source_target_pairs={{2,10},{6,14},{10,18},{14,22},{18,26},{22,30},{26,2},{30,6},{3,11}... | collective-permute-start | bytes 786440 | tf_op jit(solution)/shard_map/ppermute | solution.py:208
  13.8 0.0 collective-permute-done.refs_1_
  13.9 0.9 %collective-permute-start.1 = (bf16[2,512,128]{2,1,0:T(8,128)(2,1)S(1)}, bf16[2,512,128]{2,1,0:T(8,128)(2,1)S(1)}, u32[]{:S(2)}, u32[]{:S(2)}) collective-permute-start(bf16[2,512,128]{2,1,0:T(8,128)(2,1)S(1)} %collective-permute-done.refs_1_), channel_id=1, source_target_pairs={{0,8},{2,10},{4,12},{6,14},{8,16},{10,18},{12,20},{14,22},{16,24},... | collective-permute-start | bytes 786440 | tf_op jit(solution)/shard_map/ppermute | solution.py:208
  14.7 0.0 collective-permute-done.3.refs_5_.refs_4_
  14.7 0.0 collective-permute-done.2.refs_3_
  14.7 4.3 %shard_map.96 = (f32[512,512]{1,0:T(8,128)S(1)}, f32[512,512]{1,0:T(8,128)S(1)}, bf16[2,256,128]{2,1,0:T(8,128)(2,1)S(1)}, f32[2,256,128]{2,1,0:T(8,128)S(1)}) custom-call(s32[10,256]{1,0:T(8,128)S(1)} %get-tuple-element.25.refs_0_, bf16[2,512,128]{2,1,0:T(8,128)(2,1)S(1)} %collective-permute-done.refs_1_, ...), custom_call_target="tpu_custom_call", output_to_operand_aliasing={{0}: (6, {})} | custom-call | flops 2147483648 | bytes 2097152 | tf_op jit(solution)/shard_map/pallas_call | solution.py:108
  19.0 4.3 %shard_map.97 = (f32[512,512]{1,0:T(8,128)S(1)}, f32[512,512]{1,0:T(8,128)S(1)}, bf16[2,256,128]{2,1,0:T(8,128)(2,1)S(1)}, f32[2,256,128]{2,1,0:T(8,128)S(1)}) custom-call(s32[10,256]{1,0:T(8,128)S(1)} %get-tuple-element.25.refs_0_, bf16[2,512,128]{2,1,0:T(8,128)(2,1)S(1)} %collective-permute-done.4.refs_1_, ...), custom_call_target="tpu_custom_call", output_to_operand_aliasing={{0}: (6, {}), {1}: (7, {})} | custom-call | flops 2147483648 | bytes 2097152 | tf_op jit(solution)/shard_map/pallas_call | solution.py:108
  23.4 1.6 %collective-permute-done.1.refs_1_ = bf16[2,512,128]{2,1,0:T(8,128)(2,1)S(1)} collective-permute-done((bf16[2,512,128]{2,1,0:T(8,128)(2,1)S(1)}, bf16[2,512,128]{2,1,0:T(8,128)(2,1)S(1)}, u32[]{:S(2)}, u32[]{:S(2)}) %collective-permute-start.1) | collective-permute-done | bytes 262176 | tf_op jit(solution)/shard_map/ppermute | solution.py:208
  25.0 4.6 %shard_map.98 = (f32[512,512]{1,0:T(8,128)S(1)}, f32[512,512]{1,0:T(8,128)S(1)}, bf16[2,256,128]{2,1,0:T(8,128)(2,1)S(1)}, f32[2,256,128]{2,1,0:T(8,128)S(1)}) custom-call(s32[10,256]{1,0:T(8,128)S(1)} %get-tuple-element.25.refs_0_, bf16[2,512,128]{2,1,0:T(8,128)(2,1)S(1)} %collective-permute-done.1.refs_1_, ...), custom_call_target="tpu_custom_call", output_to_operand_aliasing={{0}: (6, {}), {1}: (7, {})} | custom-call | flops 2147483648 | bytes 2097152 | tf_op jit(solution)/shard_map/pallas_call | solution.py:108
  29.5 0.0 collective-permute-done.5.refs_2_
  29.5 2.3 %shard_map.99 = (f32[512,512]{1,0:T(8,128)S(1)}, bf16[2,256,128]{2,1,0:T(8,128)(2,1)S(1)}, f32[2,256,128]{2,1,0:T(8,128)S(1)}) custom-call(s32[10,256]{1,0:T(8,128)S(1)} %get-tuple-element.25.refs_0_, bf16[2,512,128]{2,1,0:T(8,128)(2,1)S(1)} %pad_maximum_fusion.refs_1_, ...), custom_call_target="tpu_custom_call", output_to_operand_aliasing={{0}: (5, {})} | custom-call | flops 1073741824 | bytes 2097152 | tf_op jit(solution)/shard_map/pallas_call | solution.py:108
  31.9 0.3 collective-permute-start.8
  32.1 1.2 %collective-permute-start.12 = (bf16[2,256,128]{2,1,0:T(8,128)(2,1)S(1)}, bf16[2,256,128]{2,1,0:T(8,128)(2,1)S(1)}, u32[]{:S(2)}, u32[]{:S(2)}) collective-permute-start(bf16[2,256,128]{2,1,0:T(8,128)(2,1)S(1)} %get-tuple-element.44), channel_id=1, source_target_pairs={{0,1},{1,0},{2,3},{3,2},{4,5},{5,4},{6,7},{7,6},{8,9},{9,8},{10,11... | collective-permute-start | bytes 393224 | tf_op jit(solution)/shard_map/ppermute | solution.py:214
  33.4 0.2 collective-permute-start.10
  33.6 1.3 %collective-permute-start.7 = (bf16[2,2,256,128]{3,2,1,0:T(8,128)(2,1)S(1)}, bf16[2,2,256,128]{3,2,1,0:T(8,128)(2,1)S(1)}, u32[]{:S(2)}, u32[]{:S(2)}) collective-permute-start(bf16[2,2,256,128]{3,2,1,0:T(8,128)(2,1)S(1)} %pad_maximum_fusion.1), channel_id=1, source_target_pairs={{0,1},{1,0},{2,3},{3,2},{4,5},{5,4},{6,7},{7,6},{8,9},{9,8},{10,11... | collective-permute-start | bytes 786440 | tf_op jit(solution)/shard_map/ppermute | solution.py:214
  34.9 2.5 %collective-permute-start.6 = (f32[512,512]{1,0:T(8,128)S(1)}, f32[512,512]{1,0:T(8,128)S(1)}, u32[]{:S(2)}, u32[]{:S(2)}) collective-permute-start(f32[512,512]{1,0:T(8,128)S(1)} %get-tuple-element.34), channel_id=1, source_target_pairs={{0,2},{2,0},{4,6},{6,4},{8,10},{10,8},{12,14},{14,12},{16,18},{18,... | collective-permute-start | bytes 3145736 | tf_op jit(solution)/shard_map/ppermute | solution.py:211
  37.4 0.0 collective-permute-done.8.flip8_ref
  37.5 3.3 %collective-permute-start.14 = (bf16[2,256,128]{2,1,0:T(8,128)(2,1)S(1)}, bf16[2,256,128]{2,1,0:T(8,128)(2,1)S(1)}, u32[]{:S(2)}, u32[]{:S(2)}) collective-permute-start(bf16[2,256,128]{2,1,0:T(8,128)(2,1)S(1)} %add_convert_fusion), channel_id=1, source_target_pairs={{2,18},{6,22},{10,26},{14,30},{18,2},{22,6},{26,10},{30,14},{3,19}... | collective-permute-start | bytes 393224 | tf_op jit(solution)/shard_map/ppermute | solution.py:208
  40.8 0.0 collective-permute-done.12
  40.9 2.0 %collective-permute-start.13 = (bf16[2,256,128]{2,1,0:T(8,128)(2,1)S(1)}, bf16[2,256,128]{2,1,0:T(8,128)(2,1)S(1)}, u32[]{:S(2)}, u32[]{:S(2)}) collective-permute-start(bf16[2,256,128]{2,1,0:T(8,128)(2,1)S(1)} %add_convert_fusion.1), channel_id=1, source_target_pairs={{0,20},{2,22},{4,24},{6,26},{8,28},{10,30},{12,0},{14,2},{16,4},{1... | collective-permute-start | bytes 393224 | tf_op jit(solution)/shard_map/ppermute | solution.py:208
  42.9 0.0 collective-permute-done.10
  42.9 2.2 %collective-permute-start.11 = (bf16[2,256,128]{2,1,0:T(8,128)(2,1)S(1)}, bf16[2,256,128]{2,1,0:T(8,128)(2,1)S(1)}, u32[]{:S(2)}, u32[]{:S(2)}) collective-permute-start(bf16[2,256,128]{2,1,0:T(8,128)(2,1)S(1)} %add_convert_fusion.2), channel_id=1, source_target_pairs={{0,24},{2,26},{4,28},{6,30},{8,0},{10,2},{12,4},{14,6},{16,8},{18,... | collective-permute-start | bytes 393224 | tf_op jit(solution)/shard_map/ppermute | solution.py:208
  45.1 1.8 %collective-permute-done.7 = bf16[2,2,256,128]{3,2,1,0:T(8,128)(2,1)S(1)} collective-permute-done((bf16[2,2,256,128]{3,2,1,0:T(8,128)(2,1)S(1)}, bf16[2,2,256,128]{3,2,1,0:T(8,128)(2,1)S(1)}, u32[]{:S(2)}, u32[]{:S(2)}) %collective-permute-start.7) | collective-permute-done | bytes 262176 | tf_op jit(solution)/shard_map/ppermute | solution.py:214
  46.9 1.8 %collective-permute-start.9 = (bf16[2,256,128]{2,1,0:T(8,128)(2,1)S(1)}, bf16[2,256,128]{2,1,0:T(8,128)(2,1)S(1)}, u32[]{:S(2)}, u32[]{:S(2)}) collective-permute-start(bf16[2,256,128]{2,1,0:T(8,128)(2,1)S(1)} %fusion), channel_id=1, source_target_pairs={{0,28},{2,30},{4,0},{6,2},{8,4},{10,6},{12,8},{14,10},{16,12},{18,... | collective-permute-start | bytes 393224 | tf_op jit(solution)/shard_map/ppermute | solution.py:208
  48.7 0.0 collective-permute-done.14.refs_3_
  48.7 10.9 %collective-permute-done.13.refs_2_ = bf16[2,256,128]{2,1,0:T(8,128)(2,1)S(1)} collective-permute-done((bf16[2,256,128]{2,1,0:T(8,128)(2,1)S(1)}, bf16[2,256,128]{2,1,0:T(8,128)(2,1)S(1)}, u32[]{:S(2)}, u32[]{:S(2)}) %collective-permute-start.13) | collective-permute-done | bytes 131104 | tf_op jit(solution)/shard_map/ppermute | solution.py:208
  59.6 0.0 collective-permute-done.11.refs_1_
  59.6 0.0 collective-permute-done.9.refs_0_
  59.6 0.8 %shard_map.101 = (bf16[256,128]{1,0:T(8,128)(2,1)}, bf16[256,128]{1,0:T(8,128)(2,1)}) custom-call(f32[2,256,128]{2,1,0:T(8,128)S(1)} %get-tuple-element.35.keep_ref, bf16[2,256,128]{2,1,0:T(8,128)(2,1)S(1)} %slice_bitcast_fusion.1.flip_ref, f32[2,256,128]{2,1,0:T(8,128)S(1)} %get-tuple-element.38.keep8_ref, ...), custom_call_target="tpu_custom_call" | custom-call | tf_op jit(solution)/shard_map/pallas_call | solution.py:108
  60.3 0.0 collective-permute-done.6.theirs_ref
  60.3 1.0 %shard_map.100 = bf16[512,512]{1,0:T(8,128)(2,1)} custom-call(f32[512,512]{1,0:T(8,128)S(1)} %get-tuple-element.32.mine_ref, f32[512,512]{1,0:T(8,128)S(1)} %collective-permute-done.6.theirs_ref), custom_call_target="tpu_custom_call" | custom-call | tf_op jit(solution)/shard_map/pallas_call | solution.py:108
  (7 shorter events, 0.2 us)
Async XLA Ops:
  0.6 1.2 %copy-start.3 = (bf16[512,512]{1,0:T(8,128)(2,1)S(1)}, bf16[512,512]{1,0:T(8,128)(2,1)}, u32[]{:S(2)}) copy-start(bf16[512,512]{1,0:T(8,128)(2,1)} %param.11) | copy-start | bytes 1572868
  1.8 0.9 %copy-start.4 = (bf16[512,128]{1,0:T(8,128)(2,1)S(1)}, bf16[512,128]{1,0:T(8,128)(2,1)}, u32[]{:S(2)}) copy-start(bf16[512,128]{1,0:T(8,128)(2,1)} %param.9) | copy-start | bytes 393220
  1.8 1.0 %copy-start.5 = (bf16[512,128]{1,0:T(8,128)(2,1)S(1)}, bf16[512,128]{1,0:T(8,128)(2,1)}, u32[]{:S(2)}) copy-start(bf16[512,128]{1,0:T(8,128)(2,1)} %param.8) | copy-start | bytes 393220
  1.8 2.3 %copy-start.1 = (f32[4,512]{1,0:T(4,128)S(1)}, f32[4,512]{1,0:T(4,128)}, u32[]{:S(2)}) copy-start(f32[4,512]{1,0:T(4,128)} %norm.1) | copy-start | bytes 24580
  1.9 2.2 %copy-start = (bf16[512,512]{1,0:T(8,128)(2,1)S(1)}, bf16[512,512]{1,0:T(8,128)(2,1)}, u32[]{:S(2)}) copy-start(bf16[512,512]{1,0:T(8,128)(2,1)} %output.1) | copy-start | bytes 1572868
  1.9 12.8 %collective-permute-start.2 = (bf16[512,1024]{1,0:T(8,128)(2,1)S(1)}, bf16[512,1024]{1,0:T(8,128)(2,1)S(1)}, u32[]{:S(2)}, u32[]{:S(2)}) collective-permute-start(bf16[512,1024]{1,0:T(8,128)(2,1)S(1)} %constant_dynamic-update-slice_fusion.query_grad.refs_2_), channel_id=1, source_target_pairs={{0,2},{2,0},{4,6},{6,4},{8,10},{10,8},{12,14},{14,12},{16,18},{18,... | collective-permute-start | bytes 3145736 | tf_op jit(solution)/shard_map/ppermute | solution.py:211
  2.8 1.3 %copy-start.2 = (s32[16]{0:T(128)S(1)}, s32[16]{0:T(128)}, u32[]{:S(2)}) copy-start(s32[16]{0:T(128)} %stripe.1) | copy-start | bytes 196
  2.8 7.2 %collective-permute-start.4 = (bf16[2,512,128]{2,1,0:T(8,128)(2,1)S(1)}, bf16[2,512,128]{2,1,0:T(8,128)(2,1)S(1)}, u32[]{:S(2)}, u32[]{:S(2)}) collective-permute-start(bf16[2,512,128]{2,1,0:T(8,128)(2,1)S(1)} %pad_maximum_fusion.refs_1_), channel_id=1, source_target_pairs={{0,8},{2,10},{4,12},{6,14},{8,16},{10,18},{12,20},{14,22},{16,24},... | collective-permute-start | bytes 786440 | tf_op jit(solution)/shard_map/ppermute | solution.py:208
  2.9 10.9 %collective-permute-start = (bf16[2,512,128]{2,1,0:T(8,128)(2,1)S(1)}, bf16[2,512,128]{2,1,0:T(8,128)(2,1)S(1)}, u32[]{:S(2)}, u32[]{:S(2)}) collective-permute-start(bf16[2,512,128]{2,1,0:T(8,128)(2,1)S(1)} %pad_maximum_fusion.refs_1_), channel_id=1, source_target_pairs={{0,4},{2,6},{4,8},{6,10},{8,12},{10,14},{12,16},{14,18},{16,20},{1... | collective-permute-start | bytes 786440 | tf_op jit(solution)/shard_map/ppermute | solution.py:208
  5.0 9.7 %collective-permute-start.3 = (f32[2,4,512]{2,1,0:T(4,128)S(1)}, f32[2,4,512]{2,1,0:T(4,128)S(1)}, u32[]{:S(2)}, u32[]{:S(2)}) collective-permute-start(f32[2,4,512]{2,1,0:T(4,128)S(1)} %get-tuple-element.26.refs_3_.refs_4_), channel_id=1, source_target_pairs={{0,2},{2,0},{4,6},{6,4},{8,10},{10,8},{12,14},{14,12},{16,18},{18,... | collective-permute-start | bytes 49160 | tf_op jit(solution)/shard_map/ppermute | solution.py:211
  10.1 19.4 %collective-permute-start.5 = (bf16[2,512,128]{2,1,0:T(8,128)(2,1)S(1)}, bf16[2,512,128]{2,1,0:T(8,128)(2,1)S(1)}, u32[]{:S(2)}, u32[]{:S(2)}) collective-permute-start(bf16[2,512,128]{2,1,0:T(8,128)(2,1)S(1)} %collective-permute-done.4.refs_1_), channel_id=1, source_target_pairs={{2,10},{6,14},{10,18},{14,22},{18,26},{22,30},{26,2},{30,6},{3,11}... | collective-permute-start | bytes 786440 | tf_op jit(solution)/shard_map/ppermute | solution.py:208
  13.9 11.1 %collective-permute-start.1 = (bf16[2,512,128]{2,1,0:T(8,128)(2,1)S(1)}, bf16[2,512,128]{2,1,0:T(8,128)(2,1)S(1)}, u32[]{:S(2)}, u32[]{:S(2)}) collective-permute-start(bf16[2,512,128]{2,1,0:T(8,128)(2,1)S(1)} %collective-permute-done.refs_1_), channel_id=1, source_target_pairs={{0,8},{2,10},{4,12},{6,14},{8,16},{10,18},{12,20},{14,22},{16,24},... | collective-permute-start | bytes 786440 | tf_op jit(solution)/shard_map/ppermute | solution.py:208
  31.9 5.6 %collective-permute-start.8 = (bf16[2,256,128]{2,1,0:T(8,128)(2,1)S(1)}, bf16[2,256,128]{2,1,0:T(8,128)(2,1)S(1)}, u32[]{:S(2)}, u32[]{:S(2)}) collective-permute-start(bf16[2,256,128]{2,1,0:T(8,128)(2,1)S(1)} %get-tuple-element.39), channel_id=1, source_target_pairs={{0,1},{1,0},{2,3},{3,2},{4,5},{5,4},{6,7},{7,6},{8,9},{9,8},{10,11... | collective-permute-start | bytes 393224 | tf_op jit(solution)/shard_map/ppermute | solution.py:214
  32.1 8.7 %collective-permute-start.12 = (bf16[2,256,128]{2,1,0:T(8,128)(2,1)S(1)}, bf16[2,256,128]{2,1,0:T(8,128)(2,1)S(1)}, u32[]{:S(2)}, u32[]{:S(2)}) collective-permute-start(bf16[2,256,128]{2,1,0:T(8,128)(2,1)S(1)} %get-tuple-element.44), channel_id=1, source_target_pairs={{0,1},{1,0},{2,3},{3,2},{4,5},{5,4},{6,7},{7,6},{8,9},{9,8},{10,11... | collective-permute-start | bytes 393224 | tf_op jit(solution)/shard_map/ppermute | solution.py:214
  33.4 9.5 %collective-permute-start.10 = (bf16[2,256,128]{2,1,0:T(8,128)(2,1)S(1)}, bf16[2,256,128]{2,1,0:T(8,128)(2,1)S(1)}, u32[]{:S(2)}, u32[]{:S(2)}) collective-permute-start(bf16[2,256,128]{2,1,0:T(8,128)(2,1)S(1)} %get-tuple-element.42), channel_id=1, source_target_pairs={{0,1},{1,0},{2,3},{3,2},{4,5},{5,4},{6,7},{7,6},{8,9},{9,8},{10,11... | collective-permute-start | bytes 393224 | tf_op jit(solution)/shard_map/ppermute | solution.py:214
  33.6 13.2 %collective-permute-start.7 = (bf16[2,2,256,128]{3,2,1,0:T(8,128)(2,1)S(1)}, bf16[2,2,256,128]{3,2,1,0:T(8,128)(2,1)S(1)}, u32[]{:S(2)}, u32[]{:S(2)}) collective-permute-start(bf16[2,2,256,128]{3,2,1,0:T(8,128)(2,1)S(1)} %pad_maximum_fusion.1), channel_id=1, source_target_pairs={{0,1},{1,0},{2,3},{3,2},{4,5},{5,4},{6,7},{7,6},{8,9},{9,8},{10,11... | collective-permute-start | bytes 786440 | tf_op jit(solution)/shard_map/ppermute | solution.py:214
  34.9 25.4 %collective-permute-start.6 = (f32[512,512]{1,0:T(8,128)S(1)}, f32[512,512]{1,0:T(8,128)S(1)}, u32[]{:S(2)}, u32[]{:S(2)}) collective-permute-start(f32[512,512]{1,0:T(8,128)S(1)} %get-tuple-element.34), channel_id=1, source_target_pairs={{0,2},{2,0},{4,6},{6,4},{8,10},{10,8},{12,14},{14,12},{16,18},{18,... | collective-permute-start | bytes 3145736 | tf_op jit(solution)/shard_map/ppermute | solution.py:211
  37.5 11.2 %collective-permute-start.14 = (bf16[2,256,128]{2,1,0:T(8,128)(2,1)S(1)}, bf16[2,256,128]{2,1,0:T(8,128)(2,1)S(1)}, u32[]{:S(2)}, u32[]{:S(2)}) collective-permute-start(bf16[2,256,128]{2,1,0:T(8,128)(2,1)S(1)} %add_convert_fusion), channel_id=1, source_target_pairs={{2,18},{6,22},{10,26},{14,30},{18,2},{22,6},{26,10},{30,14},{3,19}... | collective-permute-start | bytes 393224 | tf_op jit(solution)/shard_map/ppermute | solution.py:208
  40.9 18.7 %collective-permute-start.13 = (bf16[2,256,128]{2,1,0:T(8,128)(2,1)S(1)}, bf16[2,256,128]{2,1,0:T(8,128)(2,1)S(1)}, u32[]{:S(2)}, u32[]{:S(2)}) collective-permute-start(bf16[2,256,128]{2,1,0:T(8,128)(2,1)S(1)} %add_convert_fusion.1), channel_id=1, source_target_pairs={{0,20},{2,22},{4,24},{6,26},{8,28},{10,30},{12,0},{14,2},{16,4},{1... | collective-permute-start | bytes 393224 | tf_op jit(solution)/shard_map/ppermute | solution.py:208
  42.9 16.7 %collective-permute-start.11 = (bf16[2,256,128]{2,1,0:T(8,128)(2,1)S(1)}, bf16[2,256,128]{2,1,0:T(8,128)(2,1)S(1)}, u32[]{:S(2)}, u32[]{:S(2)}) collective-permute-start(bf16[2,256,128]{2,1,0:T(8,128)(2,1)S(1)} %add_convert_fusion.2), channel_id=1, source_target_pairs={{0,24},{2,26},{4,28},{6,30},{8,0},{10,2},{12,4},{14,6},{16,8},{18,... | collective-permute-start | bytes 393224 | tf_op jit(solution)/shard_map/ppermute | solution.py:208
  46.9 12.7 %collective-permute-start.9 = (bf16[2,256,128]{2,1,0:T(8,128)(2,1)S(1)}, bf16[2,256,128]{2,1,0:T(8,128)(2,1)S(1)}, u32[]{:S(2)}, u32[]{:S(2)}) collective-permute-start(bf16[2,256,128]{2,1,0:T(8,128)(2,1)S(1)} %fusion), channel_id=1, source_target_pairs={{0,28},{2,30},{4,0},{6,2},{8,4},{10,6},{12,8},{14,10},{16,12},{18,... | collective-permute-start | bytes 393224 | tf_op jit(solution)/shard_map/ppermute | solution.py:208
where the time goes:
time: 61.5 us; the launch traced here: 61.3 us
  starting transfers between devices  22.7 us (37%)
  Pallas kernels  20.4 us (33%)
  waiting for transfers between devices  15.8 us (26%)
  local copies, waits for them, and re-layouts  1.4 us (2%)
  between operations  0.81 us (1%)
    pallas_call x8, Pallas kernels, call(): pl.pallas_call(kernel, out_shape=out_shape, in_specs=[SMEM if s else vmem...  20.4 us
    ppermute x8, starting transfers between devices, shift(): return lax.ppermute(x, 'seq', route)  15.2 us
    ppermute x8, waiting for transfers between devices, shift(): return lax.ppermute(x, 'seq', route)  14 us
    ppermute x3, starting transfers between devices, flip_core(): return lax.ppermute(x, 'seq', [(i, i ^ 1) for i in range(n)])  4.48 us
    ppermute x4, starting transfers between devices, flip_head(): return lax.ppermute(x, 'head', [(0, 1), (1, 0)])  3.06 us
    ppermute x4, waiting for transfers between devices, flip_head(): return lax.ppermute(x, 'head', [(0, 1), (1, 0)])  1.8 us
    unnamed x13, local copies, waits for them, and re-layouts  1.33 us
  transfers between devices with their start and end apart: 15, of which 4 were waited for; matrix products, arithmetic and copies ran while one was open for 0% of the time, Pallas kernels for 28%

commit v1 on v0

--- a/solution.py
+++ b/solution.py
@@ -143,15 +143,19 @@
         out_ref[:, cols] = (mine_ref[cols, :] + theirs_ref[cols, :]).T.astype(out_ref.dtype)
 
 
-def final_kernel(keep_ref, flip_ref, keep8_ref, flip8_ref, *refs):
-    *backs, key_ref, value_ref = refs
+def early_kernel(keep_ref, flip_ref, keep8_ref, flip8_ref, *refs):
+    *backs, out_ref = refs
     twice = (lax.rem(lax.axis_index("seq"), 2) == 0).astype(jnp.float32)
+    total = keep_ref[...] + flip_ref[...].astype(jnp.float32)
+    total += twice * (keep8_ref[...] + flip8_ref[...].astype(jnp.float32))
+    for back in backs:
+        total += back[...].astype(jnp.float32)
+    out_ref[...] = total
+
+
+def final_kernel(early_ref, back_ref, key_ref, value_ref):
     for i, out in enumerate((key_ref, value_ref)):
-        total = keep_ref[i] + flip_ref[i].astype(jnp.float32)
-        total += twice * (keep8_ref[i] + flip8_ref[i].astype(jnp.float32))
-        for back in backs:
-            total += back[i].astype(jnp.float32)
-        out[...] = total.astype(out.dtype)
+        out[...] = (early_ref[i] + back_ref[i].astype(jnp.float32)).astype(out.dtype)
 
 
 def terms(plan, backs, kvs, opens, query_grad, level, dq_in):
@@ -258,11 +262,12 @@
     (grad_query,) = call(
         functools.partial(query_kernel, heads), [bf16((rows, width))], [dq[0], their_dq]
     )
-    grad_key, grad_value = call(
-        final_kernel,
-        [bf16((half, d))] * 2,
-        [keep0, flip0, keep8, flip8, back2, back4, back6, back8],
-    )
+    (early,) = call(
+        early_kernel,
+        [jax.ShapeDtypeStruct((2, half, d), jnp.float32)],
+        [keep0, flip0, keep8, flip8, back2, back4, back6],
+    )
+    grad_key, grad_value = call(final_kernel, [bf16((half, d))] * 2, [early, back8])
     return grad_query, grad_key, grad_value
 
 

time: 61.5 us -> 61.5 us (level)
    pallas_call x8 -> x9, Pallas kernels: 20.4 us -> 20.4 us  [call(): pl.pallas_call(kernel, out_shape=out_shape, in_specs=[SMEM if s else vmem...]
where the time goes in v1:
time: 61.5 us; the launch traced here: 61.4 us
  starting transfers between devices  22.7 us (37%)
  Pallas kernels  20.4 us (33%)
  waiting for transfers between devices  15.9 us (26%)
  local copies, waits for them, and re-layouts  1.4 us (2%)
  between operations  0.82 us (1%)
    pallas_call x9, Pallas kernels, call(): pl.pallas_call(kernel, out_shape=out_shape, in_specs=[SMEM if s else vmem...  20.4 us
    ppermute x8, starting transfers between devices, shift(): return lax.ppermute(x, 'seq', route)  15.2 us
    ppermute x8, waiting for transfers between devices, shift(): return lax.ppermute(x, 'seq', route)  14.1 us
    ppermute x3, starting transfers between devices, flip_core(): return lax.ppermute(x, 'seq', [(i, i ^ 1) for i in range(n)])  4.49 us
    ppermute x4, starting transfers between devices, flip_head(): return lax.ppermute(x, 'head', [(0, 1), (1, 0)])  3.06 us
    ppermute x4, waiting for transfers between devices, flip_head(): return lax.ppermute(x, 'head', [(0, 1), (1, 0)])  1.78 us
    unnamed x13, local copies, waits for them, and re-layouts  1.33 us
  transfers between devices with their start and end apart: 15, of which 4 were waited for; matrix products, arithmetic and copies ran while one was open for 0% of the time, Pallas kernels for 28%

profile of v1, /device:TPU:31, one launch (start us, length us, event | category | flops | bytes accessed | tf_op | source)
XLA Modules:
  0.0 61.4 jit_solution(7966855320667054521)
XLA Ops:
  0.6 0.0 copy-start.3
  0.6 1.2 %constant_dynamic-update-slice_fusion.1 = bf16[512,1024]{1,0:T(8,128)(2,1)S(1)} fusion(bf16[512,512]{1,0:T(8,128)(2,1)} %param.7), kind=kLoop, calls=%fused_computation.10 | loop fusion | bytes 1048576
  1.8 0.0 copy-done.3
  1.8 0.0 copy-start.4
  1.8 0.0 copy-start.5
  1.8 0.0 copy-start.1
  1.9 0.1 constant_dynamic-update-slice_fusion.query_grad.refs_2_
  1.9 0.0 copy-start
  1.9 0.7 %collective-permute-start.2 = (bf16[512,1024]{1,0:T(8,128)(2,1)S(1)}, bf16[512,1024]{1,0:T(8,128)(2,1)S(1)}, u32[]{:S(2)}, u32[]{:S(2)}) collective-permute-start(bf16[512,1024]{1,0:T(8,128)(2,1)S(1)} %constant_dynamic-update-slice_fusion.query_grad.refs_2_), channel_id=1, source_target_pairs={{0,2},{2,0},{4,6},{6,4},{8,10},{10,8},{12,14},{14,12},{16,18},{18,... | collective-permute-start | bytes 3145736 | tf_op jit(solution)/shard_map/ppermute | solution.py:215
  2.7 0.1 copy-done.4
  2.7 0.1 copy-done.5
  2.8 0.0 copy-start.2
  2.8 0.1 collective-permute-start.4
  2.9 1.2 %collective-permute-start = (bf16[2,512,128]{2,1,0:T(8,128)(2,1)S(1)}, bf16[2,512,128]{2,1,0:T(8,128)(2,1)S(1)}, u32[]{:S(2)}, u32[]{:S(2)}) collective-permute-start(bf16[2,512,128]{2,1,0:T(8,128)(2,1)S(1)} %pad_maximum_fusion.refs_1_), channel_id=1, source_target_pairs={{0,4},{2,6},{4,8},{6,10},{8,12},{10,14},{12,16},{14,18},{16,20},{1... | collective-permute-start | bytes 786440 | tf_op jit(solution)/shard_map/ppermute | solution.py:212
  4.1 0.0 copy-done.1
  4.1 0.0 copy-done
  4.1 0.0 copy-done.2
  4.1 0.9 %shard_map.94 = (f32[2,4,512]{2,1,0:T(4,128)S(1)}, s32[10,256]{1,0:T(8,128)S(1)}) custom-call(s32[16]{0:T(128)S(1)} %copy-done.2, bf16[512,1024]{1,0:T(8,128)(2,1)S(1)} %constant_dynamic-update-slice_fusion.query_grad.refs_2_, bf16[512,512]{1,0:T(8,128)(2,1)S(1)} %copy-done, f32[4,512]{1,0:T(4,128)S(1)} %copy-done.1), custom_call_target="tpu_custom_call" | custom-call | tf_op jit(solution)/shard_map/pallas_call | solution.py:108
  5.0 1.3 %collective-permute-start.3 = (f32[2,4,512]{2,1,0:T(4,128)S(1)}, f32[2,4,512]{2,1,0:T(4,128)S(1)}, u32[]{:S(2)}, u32[]{:S(2)}) collective-permute-start(f32[2,4,512]{2,1,0:T(4,128)S(1)} %get-tuple-element.26.refs_3_.refs_4_), channel_id=1, source_target_pairs={{0,2},{2,0},{4,6},{6,4},{8,10},{10,8},{12,14},{14,12},{16,18},{18,... | collective-permute-start | bytes 49160 | tf_op jit(solution)/shard_map/ppermute | solution.py:215
  6.3 2.2 %shard_map.95 = (f32[512,512]{1,0:T(8,128)S(1)}, bf16[2,256,128]{2,1,0:T(8,128)(2,1)S(1)}, f32[2,256,128]{2,1,0:T(8,128)S(1)}) custom-call(s32[10,256]{1,0:T(8,128)S(1)} %get-tuple-element.25.refs_0_, bf16[2,512,128]{2,1,0:T(8,128)(2,1)S(1)} %pad_maximum_fusion.refs_1_, bf16[512,1024]{1,0:T(8,128)(2,1)S(1)} %constant_dynamic-update-slice_fusion.query_grad.refs_2_, ...), custom_call_target="tpu_custom_call" | custom-call | flops 1073741824 | bytes 2097152 | tf_op jit(solution)/shard_map/pallas_call | solution.py:108
  8.5 1.5 %collective-permute-done.4.refs_1_ = bf16[2,512,128]{2,1,0:T(8,128)(2,1)S(1)} collective-permute-done((bf16[2,512,128]{2,1,0:T(8,128)(2,1)S(1)}, bf16[2,512,128]{2,1,0:T(8,128)(2,1)S(1)}, u32[]{:S(2)}, u32[]{:S(2)}) %collective-permute-start.4) | collective-permute-done | bytes 262176 | tf_op jit(solution)/shard_map/ppermute | solution.py:212
  10.1 3.8 %collective-permute-start.5 = (bf16[2,512,128]{2,1,0:T(8,128)(2,1)S(1)}, bf16[2,512,128]{2,1,0:T(8,128)(2,1)S(1)}, u32[]{:S(2)}, u32[]{:S(2)}) collective-permute-start(bf16[2,512,128]{2,1,0:T(8,128)(2,1)S(1)} %collective-permute-done.4.refs_1_), channel_id=1, source_target_pairs={{2,10},{6,14},{10,18},{14,22},{18,26},{22,30},{26,2},{30,6},{3,11}... | collective-permute-start | bytes 786440 | tf_op jit(solution)/shard_map/ppermute | solution.py:212
  13.8 0.0 collective-permute-done.refs_1_
  13.9 0.9 %collective-permute-start.1 = (bf16[2,512,128]{2,1,0:T(8,128)(2,1)S(1)}, bf16[2,512,128]{2,1,0:T(8,128)(2,1)S(1)}, u32[]{:S(2)}, u32[]{:S(2)}) collective-permute-start(bf16[2,512,128]{2,1,0:T(8,128)(2,1)S(1)} %collective-permute-done.refs_1_), channel_id=1, source_target_pairs={{0,8},{2,10},{4,12},{6,14},{8,16},{10,18},{12,20},{14,22},{16,24},... | collective-permute-start | bytes 786440 | tf_op jit(solution)/shard_map/ppermute | solution.py:212
  14.7 0.0 collective-permute-done.3.refs_5_.refs_4_
  14.7 0.0 collective-permute-done.2.refs_3_
  14.7 4.3 %shard_map.96 = (f32[512,512]{1,0:T(8,128)S(1)}, f32[512,512]{1,0:T(8,128)S(1)}, bf16[2,256,128]{2,1,0:T(8,128)(2,1)S(1)}, f32[2,256,128]{2,1,0:T(8,128)S(1)}) custom-call(s32[10,256]{1,0:T(8,128)S(1)} %get-tuple-element.25.refs_0_, bf16[2,512,128]{2,1,0:T(8,128)(2,1)S(1)} %collective-permute-done.refs_1_, ...), custom_call_target="tpu_custom_call", output_to_operand_aliasing={{0}: (6, {})} | custom-call | flops 2147483648 | bytes 2097152 | tf_op jit(solution)/shard_map/pallas_call | solution.py:108
  19.0 4.3 %shard_map.97 = (f32[512,512]{1,0:T(8,128)S(1)}, f32[512,512]{1,0:T(8,128)S(1)}, bf16[2,256,128]{2,1,0:T(8,128)(2,1)S(1)}, f32[2,256,128]{2,1,0:T(8,128)S(1)}) custom-call(s32[10,256]{1,0:T(8,128)S(1)} %get-tuple-element.25.refs_0_, bf16[2,512,128]{2,1,0:T(8,128)(2,1)S(1)} %collective-permute-done.4.refs_1_, ...), custom_call_target="tpu_custom_call", output_to_operand_aliasing={{0}: (6, {}), {1}: (7, {})} | custom-call | flops 2147483648 | bytes 2097152 | tf_op jit(solution)/shard_map/pallas_call | solution.py:108
  23.4 1.6 %collective-permute-done.1.refs_1_ = bf16[2,512,128]{2,1,0:T(8,128)(2,1)S(1)} collective-permute-done((bf16[2,512,128]{2,1,0:T(8,128)(2,1)S(1)}, bf16[2,512,128]{2,1,0:T(8,128)(2,1)S(1)}, u32[]{:S(2)}, u32[]{:S(2)}) %collective-permute-start.1) | collective-permute-done | bytes 262176 | tf_op jit(solution)/shard_map/ppermute | solution.py:212
  25.0 4.6 %shard_map.98 = (f32[512,512]{1,0:T(8,128)S(1)}, f32[512,512]{1,0:T(8,128)S(1)}, bf16[2,256,128]{2,1,0:T(8,128)(2,1)S(1)}, f32[2,256,128]{2,1,0:T(8,128)S(1)}) custom-call(s32[10,256]{1,0:T(8,128)S(1)} %get-tuple-element.25.refs_0_, bf16[2,512,128]{2,1,0:T(8,128)(2,1)S(1)} %collective-permute-done.1.refs_1_, ...), custom_call_target="tpu_custom_call", output_to_operand_aliasing={{0}: (6, {}), {1}: (7, {})} | custom-call | flops 2147483648 | bytes 2097152 | tf_op jit(solution)/shard_map/pallas_call | solution.py:108
  29.5 0.0 collective-permute-done.5.refs_2_
  29.5 2.3 %shard_map.99 = (f32[512,512]{1,0:T(8,128)S(1)}, bf16[2,256,128]{2,1,0:T(8,128)(2,1)S(1)}, f32[2,256,128]{2,1,0:T(8,128)S(1)}) custom-call(s32[10,256]{1,0:T(8,128)S(1)} %get-tuple-element.25.refs_0_, bf16[2,512,128]{2,1,0:T(8,128)(2,1)S(1)} %pad_maximum_fusion.refs_1_, ...), custom_call_target="tpu_custom_call", output_to_operand_aliasing={{0}: (5, {})} | custom-call | flops 1073741824 | bytes 2097152 | tf_op jit(solution)/shard_map/pallas_call | solution.py:108
  31.9 0.3 collective-permute-start.8
  32.1 1.2 %collective-permute-start.12 = (bf16[2,256,128]{2,1,0:T(8,128)(2,1)S(1)}, bf16[2,256,128]{2,1,0:T(8,128)(2,1)S(1)}, u32[]{:S(2)}, u32[]{:S(2)}) collective-permute-start(bf16[2,256,128]{2,1,0:T(8,128)(2,1)S(1)} %get-tuple-element.44), channel_id=1, source_target_pairs={{0,1},{1,0},{2,3},{3,2},{4,5},{5,4},{6,7},{7,6},{8,9},{9,8},{10,11... | collective-permute-start | bytes 393224 | tf_op jit(solution)/shard_map/ppermute | solution.py:218
  33.4 0.2 collective-permute-start.10
  33.6 1.3 %collective-permute-start.7 = (bf16[2,2,256,128]{3,2,1,0:T(8,128)(2,1)S(1)}, bf16[2,2,256,128]{3,2,1,0:T(8,128)(2,1)S(1)}, u32[]{:S(2)}, u32[]{:S(2)}) collective-permute-start(bf16[2,2,256,128]{3,2,1,0:T(8,128)(2,1)S(1)} %pad_maximum_fusion.1), channel_id=1, source_target_pairs={{0,1},{1,0},{2,3},{3,2},{4,5},{5,4},{6,7},{7,6},{8,9},{9,8},{10,11... | collective-permute-start | bytes 786440 | tf_op jit(solution)/shard_map/ppermute | solution.py:218
  34.9 2.5 %collective-permute-start.6 = (f32[512,512]{1,0:T(8,128)S(1)}, f32[512,512]{1,0:T(8,128)S(1)}, u32[]{:S(2)}, u32[]{:S(2)}) collective-permute-start(f32[512,512]{1,0:T(8,128)S(1)} %get-tuple-element.34), channel_id=1, source_target_pairs={{0,2},{2,0},{4,6},{6,4},{8,10},{10,8},{12,14},{14,12},{16,18},{18,... | collective-permute-start | bytes 3145736 | tf_op jit(solution)/shard_map/ppermute | solution.py:215
  37.4 0.0 collective-permute-done.8.flip8_ref
  37.5 3.3 %collective-permute-start.14 = (bf16[2,256,128]{2,1,0:T(8,128)(2,1)S(1)}, bf16[2,256,128]{2,1,0:T(8,128)(2,1)S(1)}, u32[]{:S(2)}, u32[]{:S(2)}) collective-permute-start(bf16[2,256,128]{2,1,0:T(8,128)(2,1)S(1)} %add_convert_fusion), channel_id=1, source_target_pairs={{2,18},{6,22},{10,26},{14,30},{18,2},{22,6},{26,10},{30,14},{3,19}... | collective-permute-start | bytes 393224 | tf_op jit(solution)/shard_map/ppermute | solution.py:212
  40.8 0.0 collective-permute-done.12
  40.8 2.0 %collective-permute-start.13 = (bf16[2,256,128]{2,1,0:T(8,128)(2,1)S(1)}, bf16[2,256,128]{2,1,0:T(8,128)(2,1)S(1)}, u32[]{:S(2)}, u32[]{:S(2)}) collective-permute-start(bf16[2,256,128]{2,1,0:T(8,128)(2,1)S(1)} %add_convert_fusion.1), channel_id=1, source_target_pairs={{0,20},{2,22},{4,24},{6,26},{8,28},{10,30},{12,0},{14,2},{16,4},{1... | collective-permute-start | bytes 393224 | tf_op jit(solution)/shard_map/ppermute | solution.py:212
  42.9 0.0 collective-permute-done.10
  42.9 2.2 %collective-permute-start.11 = (bf16[2,256,128]{2,1,0:T(8,128)(2,1)S(1)}, bf16[2,256,128]{2,1,0:T(8,128)(2,1)S(1)}, u32[]{:S(2)}, u32[]{:S(2)}) collective-permute-start(bf16[2,256,128]{2,1,0:T(8,128)(2,1)S(1)} %add_convert_fusion.2), channel_id=1, source_target_pairs={{0,24},{2,26},{4,28},{6,30},{8,0},{10,2},{12,4},{14,6},{16,8},{18,... | collective-permute-start | bytes 393224 | tf_op jit(solution)/shard_map/ppermute | solution.py:212
  45.1 1.8 %collective-permute-done.7 = bf16[2,2,256,128]{3,2,1,0:T(8,128)(2,1)S(1)} collective-permute-done((bf16[2,2,256,128]{3,2,1,0:T(8,128)(2,1)S(1)}, bf16[2,2,256,128]{3,2,1,0:T(8,128)(2,1)S(1)}, u32[]{:S(2)}, u32[]{:S(2)}) %collective-permute-start.7) | collective-permute-done | bytes 262176 | tf_op jit(solution)/shard_map/ppermute | solution.py:218
  46.9 1.8 %collective-permute-start.9 = (bf16[2,256,128]{2,1,0:T(8,128)(2,1)S(1)}, bf16[2,256,128]{2,1,0:T(8,128)(2,1)S(1)}, u32[]{:S(2)}, u32[]{:S(2)}) collective-permute-start(bf16[2,256,128]{2,1,0:T(8,128)(2,1)S(1)} %fusion), channel_id=1, source_target_pairs={{0,28},{2,30},{4,0},{6,2},{8,4},{10,6},{12,8},{14,10},{16,12},{18,... | collective-permute-start | bytes 393224 | tf_op jit(solution)/shard_map/ppermute | solution.py:212
  48.6 10.9 %collective-permute-done.13.refs_2_ = bf16[2,256,128]{2,1,0:T(8,128)(2,1)S(1)} collective-permute-done((bf16[2,256,128]{2,1,0:T(8,128)(2,1)S(1)}, bf16[2,256,128]{2,1,0:T(8,128)(2,1)S(1)}, u32[]{:S(2)}, u32[]{:S(2)}) %collective-permute-start.13) | collective-permute-done | bytes 131104 | tf_op jit(solution)/shard_map/ppermute | solution.py:212
  59.6 0.0 collective-permute-done.11.refs_1_
  59.6 0.0 collective-permute-done.9.refs_0_
  59.6 0.1 shard_map.101.early_ref
  59.7 0.0 collective-permute-done.14.back_ref
  59.7 0.7 %shard_map.102 = (bf16[256,128]{1,0:T(8,128)(2,1)}, bf16[256,128]{1,0:T(8,128)(2,1)}) custom-call(f32[2,256,128]{2,1,0:T(8,128)S(1)} %shard_map.101.early_ref, bf16[2,256,128]{2,1,0:T(8,128)(2,1)S(1)} %collective-permute-done.14.back_ref), custom_call_target="tpu_custom_call" | custom-call | tf_op jit(solution)/shard_map/pallas_call | solution.py:108
  60.4 0.0 collective-permute-done.6.theirs_ref
  60.4 1.0 %shard_map.100 = bf16[512,512]{1,0:T(8,128)(2,1)} custom-call(f32[512,512]{1,0:T(8,128)S(1)} %get-tuple-element.32.mine_ref, f32[512,512]{1,0:T(8,128)S(1)} %collective-permute-done.6.theirs_ref), custom_call_target="tpu_custom_call" | custom-call | tf_op jit(solution)/shard_map/pallas_call | solution.py:108
  (7 shorter events, 0.2 us)
Async XLA Ops:
  0.6 1.2 %copy-start.3 = (bf16[512,512]{1,0:T(8,128)(2,1)S(1)}, bf16[512,512]{1,0:T(8,128)(2,1)}, u32[]{:S(2)}) copy-start(bf16[512,512]{1,0:T(8,128)(2,1)} %param.11) | copy-start | bytes 1572868
  1.8 0.9 %copy-start.4 = (bf16[512,128]{1,0:T(8,128)(2,1)S(1)}, bf16[512,128]{1,0:T(8,128)(2,1)}, u32[]{:S(2)}) copy-start(bf16[512,128]{1,0:T(8,128)(2,1)} %param.9) | copy-start | bytes 393220
  1.8 1.0 %copy-start.5 = (bf16[512,128]{1,0:T(8,128)(2,1)S(1)}, bf16[512,128]{1,0:T(8,128)(2,1)}, u32[]{:S(2)}) copy-start(bf16[512,128]{1,0:T(8,128)(2,1)} %param.8) | copy-start | bytes 393220
  1.8 2.3 %copy-start.1 = (f32[4,512]{1,0:T(4,128)S(1)}, f32[4,512]{1,0:T(4,128)}, u32[]{:S(2)}) copy-start(f32[4,512]{1,0:T(4,128)} %norm.1) | copy-start | bytes 24580
  1.9 2.2 %copy-start = (bf16[512,512]{1,0:T(8,128)(2,1)S(1)}, bf16[512,512]{1,0:T(8,128)(2,1)}, u32[]{:S(2)}) copy-start(bf16[512,512]{1,0:T(8,128)(2,1)} %output.1) | copy-start | bytes 1572868
  1.9 12.8 %collective-permute-start.2 = (bf16[512,1024]{1,0:T(8,128)(2,1)S(1)}, bf16[512,1024]{1,0:T(8,128)(2,1)S(1)}, u32[]{:S(2)}, u32[]{:S(2)}) collective-permute-start(bf16[512,1024]{1,0:T(8,128)(2,1)S(1)} %constant_dynamic-update-slice_fusion.query_grad.refs_2_), channel_id=1, source_target_pairs={{0,2},{2,0},{4,6},{6,4},{8,10},{10,8},{12,14},{14,12},{16,18},{18,... | collective-permute-start | bytes 3145736 | tf_op jit(solution)/shard_map/ppermute | solution.py:215
  2.8 1.3 %copy-start.2 = (s32[16]{0:T(128)S(1)}, s32[16]{0:T(128)}, u32[]{:S(2)}) copy-start(s32[16]{0:T(128)} %stripe.1) | copy-start | bytes 196
  2.8 7.2 %collective-permute-start.4 = (bf16[2,512,128]{2,1,0:T(8,128)(2,1)S(1)}, bf16[2,512,128]{2,1,0:T(8,128)(2,1)S(1)}, u32[]{:S(2)}, u32[]{:S(2)}) collective-permute-start(bf16[2,512,128]{2,1,0:T(8,128)(2,1)S(1)} %pad_maximum_fusion.refs_1_), channel_id=1, source_target_pairs={{0,8},{2,10},{4,12},{6,14},{8,16},{10,18},{12,20},{14,22},{16,24},... | collective-permute-start | bytes 786440 | tf_op jit(solution)/shard_map/ppermute | solution.py:212
  2.9 10.9 %collective-permute-start = (bf16[2,512,128]{2,1,0:T(8,128)(2,1)S(1)}, bf16[2,512,128]{2,1,0:T(8,128)(2,1)S(1)}, u32[]{:S(2)}, u32[]{:S(2)}) collective-permute-start(bf16[2,512,128]{2,1,0:T(8,128)(2,1)S(1)} %pad_maximum_fusion.refs_1_), channel_id=1, source_target_pairs={{0,4},{2,6},{4,8},{6,10},{8,12},{10,14},{12,16},{14,18},{16,20},{1... | collective-permute-start | bytes 786440 | tf_op jit(solution)/shard_map/ppermute | solution.py:212
  5.0 9.7 %collective-permute-start.3 = (f32[2,4,512]{2,1,0:T(4,128)S(1)}, f32[2,4,512]{2,1,0:T(4,128)S(1)}, u32[]{:S(2)}, u32[]{:S(2)}) collective-permute-start(f32[2,4,512]{2,1,0:T(4,128)S(1)} %get-tuple-element.26.refs_3_.refs_4_), channel_id=1, source_target_pairs={{0,2},{2,0},{4,6},{6,4},{8,10},{10,8},{12,14},{14,12},{16,18},{18,... | collective-permute-start | bytes 49160 | tf_op jit(solution)/shard_map/ppermute | solution.py:215
  10.1 19.4 %collective-permute-start.5 = (bf16[2,512,128]{2,1,0:T(8,128)(2,1)S(1)}, bf16[2,512,128]{2,1,0:T(8,128)(2,1)S(1)}, u32[]{:S(2)}, u32[]{:S(2)}) collective-permute-start(bf16[2,512,128]{2,1,0:T(8,128)(2,1)S(1)} %collective-permute-done.4.refs_1_), channel_id=1, source_target_pairs={{2,10},{6,14},{10,18},{14,22},{18,26},{22,30},{26,2},{30,6},{3,11}... | collective-permute-start | bytes 786440 | tf_op jit(solution)/shard_map/ppermute | solution.py:212
  13.9 11.1 %collective-permute-start.1 = (bf16[2,512,128]{2,1,0:T(8,128)(2,1)S(1)}, bf16[2,512,128]{2,1,0:T(8,128)(2,1)S(1)}, u32[]{:S(2)}, u32[]{:S(2)}) collective-permute-start(bf16[2,512,128]{2,1,0:T(8,128)(2,1)S(1)} %collective-permute-done.refs_1_), channel_id=1, source_target_pairs={{0,8},{2,10},{4,12},{6,14},{8,16},{10,18},{12,20},{14,22},{16,24},... | collective-permute-start | bytes 786440 | tf_op jit(solution)/shard_map/ppermute | solution.py:212
  31.9 5.6 %collective-permute-start.8 = (bf16[2,256,128]{2,1,0:T(8,128)(2,1)S(1)}, bf16[2,256,128]{2,1,0:T(8,128)(2,1)S(1)}, u32[]{:S(2)}, u32[]{:S(2)}) collective-permute-start(bf16[2,256,128]{2,1,0:T(8,128)(2,1)S(1)} %get-tuple-element.39), channel_id=1, source_target_pairs={{0,1},{1,0},{2,3},{3,2},{4,5},{5,4},{6,7},{7,6},{8,9},{9,8},{10,11... | collective-permute-start | bytes 393224 | tf_op jit(solution)/shard_map/ppermute | solution.py:218
  32.1 8.6 %collective-permute-start.12 = (bf16[2,256,128]{2,1,0:T(8,128)(2,1)S(1)}, bf16[2,256,128]{2,1,0:T(8,128)(2,1)S(1)}, u32[]{:S(2)}, u32[]{:S(2)}) collective-permute-start(bf16[2,256,128]{2,1,0:T(8,128)(2,1)S(1)} %get-tuple-element.44), channel_id=1, source_target_pairs={{0,1},{1,0},{2,3},{3,2},{4,5},{5,4},{6,7},{7,6},{8,9},{9,8},{10,11... | collective-permute-start | bytes 393224 | tf_op jit(solution)/shard_map/ppermute | solution.py:218
  33.4 9.5 %collective-permute-start.10 = (bf16[2,256,128]{2,1,0:T(8,128)(2,1)S(1)}, bf16[2,256,128]{2,1,0:T(8,128)(2,1)S(1)}, u32[]{:S(2)}, u32[]{:S(2)}) collective-permute-start(bf16[2,256,128]{2,1,0:T(8,128)(2,1)S(1)} %get-tuple-element.42), channel_id=1, source_target_pairs={{0,1},{1,0},{2,3},{3,2},{4,5},{5,4},{6,7},{7,6},{8,9},{9,8},{10,11... | collective-permute-start | bytes 393224 | tf_op jit(solution)/shard_map/ppermute | solution.py:218
  33.6 13.2 %collective-permute-start.7 = (bf16[2,2,256,128]{3,2,1,0:T(8,128)(2,1)S(1)}, bf16[2,2,256,128]{3,2,1,0:T(8,128)(2,1)S(1)}, u32[]{:S(2)}, u32[]{:S(2)}) collective-permute-start(bf16[2,2,256,128]{3,2,1,0:T(8,128)(2,1)S(1)} %pad_maximum_fusion.1), channel_id=1, source_target_pairs={{0,1},{1,0},{2,3},{3,2},{4,5},{5,4},{6,7},{7,6},{8,9},{9,8},{10,11... | collective-permute-start | bytes 786440 | tf_op jit(solution)/shard_map/ppermute | solution.py:218
  34.9 25.4 %collective-permute-start.6 = (f32[512,512]{1,0:T(8,128)S(1)}, f32[512,512]{1,0:T(8,128)S(1)}, u32[]{:S(2)}, u32[]{:S(2)}) collective-permute-start(f32[512,512]{1,0:T(8,128)S(1)} %get-tuple-element.34), channel_id=1, source_target_pairs={{0,2},{2,0},{4,6},{6,4},{8,10},{10,8},{12,14},{14,12},{16,18},{18,... | collective-permute-start | bytes 3145736 | tf_op jit(solution)/shard_map/ppermute | solution.py:215
  37.5 22.2 %collective-permute-start.14 = (bf16[2,256,128]{2,1,0:T(8,128)(2,1)S(1)}, bf16[2,256,128]{2,1,0:T(8,128)(2,1)S(1)}, u32[]{:S(2)}, u32[]{:S(2)}) collective-permute-start(bf16[2,256,128]{2,1,0:T(8,128)(2,1)S(1)} %add_convert_fusion), channel_id=1, source_target_pairs={{2,18},{6,22},{10,26},{14,30},{18,2},{22,6},{26,10},{30,14},{3,19}... | collective-permute-start | bytes 393224 | tf_op jit(solution)/shard_map/ppermute | solution.py:212
  40.8 18.7 %collective-permute-start.13 = (bf16[2,256,128]{2,1,0:T(8,128)(2,1)S(1)}, bf16[2,256,128]{2,1,0:T(8,128)(2,1)S(1)}, u32[]{:S(2)}, u32[]{:S(2)}) collective-permute-start(bf16[2,256,128]{2,1,0:T(8,128)(2,1)S(1)} %add_convert_fusion.1), channel_id=1, source_target_pairs={{0,20},{2,22},{4,24},{6,26},{8,28},{10,30},{12,0},{14,2},{16,4},{1... | collective-permute-start | bytes 393224 | tf_op jit(solution)/shard_map/ppermute | solution.py:212
  42.9 16.7 %collective-permute-start.11 = (bf16[2,256,128]{2,1,0:T(8,128)(2,1)S(1)}, bf16[2,256,128]{2,1,0:T(8,128)(2,1)S(1)}, u32[]{:S(2)}, u32[]{:S(2)}) collective-permute-start(bf16[2,256,128]{2,1,0:T(8,128)(2,1)S(1)} %add_convert_fusion.2), channel_id=1, source_target_pairs={{0,24},{2,26},{4,28},{6,30},{8,0},{10,2},{12,4},{14,6},{16,8},{18,... | collective-permute-start | bytes 393224 | tf_op jit(solution)/shard_map/ppermute | solution.py:212
  46.9 12.7 %collective-permute-start.9 = (bf16[2,256,128]{2,1,0:T(8,128)(2,1)S(1)}, bf16[2,256,128]{2,1,0:T(8,128)(2,1)S(1)}, u32[]{:S(2)}, u32[]{:S(2)}) collective-permute-start(bf16[2,256,128]{2,1,0:T(8,128)(2,1)S(1)} %fusion), channel_id=1, source_target_pairs={{0,28},{2,30},{4,0},{6,2},{8,4},{10,6},{12,8},{14,10},{16,12},{18,... | collective-permute-start | bytes 393224 | tf_op jit(solution)/shard_map/ppermute | solution.py:212
